TPU v7x, 32 devices: a whole 2x2x4 slice. The times are simulated.
32 devices in a mesh: seq: 2 (over core), heads: 4 (over y, x), batch: 4 (over z).
Axes of the slice: x: 2, y: 2, z: 4, core: 2. Of those that a mesh axis runs over, the one named last changes fastest.
Arguments:
- queries: bfloat16 [4, 512, 8192], P('batch', 'seq', 'heads'), may hold values from -160 to 160
- keys: bfloat16 [4, 512, 1024], P('batch', 'seq', 'heads'), may hold values from -7 to 7
- values: bfloat16 [4, 512, 1024], P('batch', 'seq', 'heads'), may hold values from -6 to 6
- doc_lengths: int32 [4, 16], P('batch'), may hold values from 1 to 384, 512 in all within a row
- out_weight: bfloat16 [8192, 8192], P('heads', 'batch'), may hold values from -0.0625 to 0.0625
Outputs:
- projected: bfloat16 [4, 512, 8192], P('heads', 'seq', 'batch')
Inputs may be any that keep to these rules, and one draw needn't show every extreme that they name: `doc_lengths`: each row sums to 512; no document is longer than 384 tokens and one is exactly 384.
All inputs are finite; a program needn't handle non-finite values.
Results may differ from a plain program's by a relative error of at most 0.012.
Values may be sent and summed in bfloat16 or wider, within the bound.
A program may use at most 64 MiB of HBM per device.

v0:
```python
import functools

import jax
import jax.numpy as jnp
from jax import lax
from jax.experimental import pallas as pl
from jax.experimental.pallas import tpu as pltpu
from jax.sharding import PartitionSpec as P

HEAD_WIDTH = 128
DOCS = 16
PIECES = 4
LAG = 2
STACK = 4
COLS = 512
MESH = pl.DeviceIdType.MESH


def kernel(
    sizes, q_ref, k_ref, v_ref, len_ref, w_hbm, out_ref,
    w_ref, keys, vals, gath, stage, incoming,
    w_sem, kv_send, kv_recv, z_send, z_recv, c_send, c_recv,
):
    seqs, groups, n, reach = sizes
    shard_len, q_width = q_ref.shape[1], q_ref.shape[2]
    kv_heads = k_ref.shape[2] // HEAD_WIDTH
    per_kv = q_width // k_ref.shape[2]
    rows = shard_len // PIECES
    slots = n * PIECES
    half = w_ref.shape[1] // 2
    key_count = keys.shape[0]

    me = lax.axis_index("seq")
    head = lax.axis_index("heads")
    b = lax.axis_index("batch")

    def ring(h):
        return h + h // 2 - 2 * (h // 3) if groups == 4 else h

    place = ring(head)
    ahead = ring(lax.rem(place + 1, groups))
    behind = ring(lax.rem(place + groups - 1, groups))

    w_copy = pltpu.make_async_copy(w_hbm, w_ref, w_sem)
    w_copy.start()

    barrier = pltpu.get_barrier_semaphore()

    def greet(axis, index):
        pl.semaphore_signal(barrier, inc=1, device_id={axis: index}, device_id_type=MESH)

    greet("heads", ahead)
    greet("heads", behind)
    expected = 2
    for cond, index in ((b > 0, b - 1), (b < n - 1, b + 1)):
        expected = expected + cond.astype(jnp.int32)
        pl.when(cond)(functools.partial(greet, "batch", index))
    for d in range(1, reach + 1):
        for cond, index in ((me >= d, me - d), (me + d < seqs, me + d)):
            expected = expected + cond.astype(jnp.int32)
            pl.when(cond)(functools.partial(greet, "seq", index))
    pl.semaphore_wait(barrier, expected)

    def kv_copies(d, target):
        spot = pl.ds((reach - d) * shard_len, shard_len)
        return [
            pltpu.make_async_remote_copy(
                src_ref=src.at[0], dst_ref=dst.at[spot],
                send_sem=kv_send.at[i, d - 1], recv_sem=kv_recv.at[i, d - 1],
                device_id={"seq": target}, device_id_type=MESH,
            )
            for i, (src, dst) in enumerate(((k_ref, keys), (v_ref, vals)))
        ]

    for d in range(1, reach + 1):
        @pl.when(me + d < seqs)
        def _():
            for copy in kv_copies(d, me + d):
                copy.start()

    keys[pl.ds(reach * shard_len, shard_len), :] = k_ref[0]
    vals[pl.ds(reach * shard_len, shard_len), :] = v_ref[0]
    for d in range(1, reach + 1):
        @pl.when(me < d)
        def _():
            spot = pl.ds((reach - d) * shard_len, shard_len)
            keys[spot, :] = jnp.zeros((shard_len, keys.shape[1]), keys.dtype)
            vals[spot, :] = jnp.zeros((shard_len, vals.shape[1]), vals.dtype)

    for d in range(1, reach + 1):
        @pl.when(me >= d)
        def _():
            for copy in kv_copies(d, me - d):
                copy.wait_recv()

    def z_copy(way, source, piece):
        spot = pl.ds(pl.multiple_of(piece * rows, rows), rows)
        return pltpu.make_async_remote_copy(
            src_ref=gath.at[source, spot], dst_ref=gath.at[source, spot],
            send_sem=z_send.at[way, source, piece], recv_sem=z_recv.at[source, piece],
            device_id={"batch": b + 1 if way == 0 else b - 1}, device_id_type=MESH,
        )

    def goes(way, source):
        if way == 0:
            return (source <= b) & (b < n - 1)
        return (source >= b) & (b > 0)

    def pass_on(source, piece):
        for way in range(2):
            @pl.when(goes(way, source))
            def _():
                z_copy(way, source, piece).start()

    factor = HEAD_WIDTH ** (-0.5)
    shard_start = me * shard_len
    first_key = shard_start - reach * shard_len

    def attend(piece, _):
        base = pl.multiple_of(piece * rows, rows)
        row_pos = shard_start + base + lax.broadcasted_iota(jnp.int32, (rows, HEAD_WIDTH), 0)
        start = jnp.zeros((rows, HEAD_WIDTH), jnp.int32)
        end = jnp.int32(0)
        for d in range(DOCS):
            end = end + len_ref[0, d]
            start = jnp.where(row_pos >= end, end, start)
        key_pos = first_key + lax.broadcasted_iota(jnp.int32, (rows, key_count), 1)
        allowed = (key_pos >= start[:, :1]) & (key_pos <= row_pos[:, :1])
        bias = jnp.where(allowed, 0.0, -jnp.inf).astype(jnp.float32)
        bias = jnp.concatenate([bias] * STACK, axis=0)
        for first in range(0, kv_heads * per_kv, STACK):
            g = first // per_kv
            gcols = slice(g * HEAD_WIDTH, (g + 1) * HEAD_WIDTH)
            q = jnp.concatenate(
                [
                    q_ref[0, pl.ds(base, rows), j * HEAD_WIDTH:(j + 1) * HEAD_WIDTH]
                    for j in range(first, first + STACK)
                ],
                axis=0,
            )
            scores = lax.dot_general(
                q, keys[:, gcols], (((1,), (1,)), ((), ())),
                preferred_element_type=jnp.float32,
            ) * factor + bias
            weights = jnp.exp(scores - jnp.max(scores, axis=1, keepdims=True))
            total = jnp.sum(weights, axis=1, keepdims=True)
            summed = jnp.dot(
                weights.astype(jnp.bfloat16), vals[:, gcols],
                preferred_element_type=jnp.float32,
            )
            result = (summed / total).astype(jnp.bfloat16)
            for i in range(STACK):
                j = first + i
                gath[b, pl.ds(base, rows), j * HEAD_WIDTH:(j + 1) * HEAD_WIDTH] = (
                    result[i * rows:(i + 1) * rows]
                )
        pass_on(b, piece)
        return 0

    lax.fori_loop(0, PIECES, attend, 0)
    w_copy.wait()

    both = jnp.minimum(b, n - 1 - b)

    def slot_of(slot):
        u = jnp.maximum(slot - PIECES, 0)
        v = jnp.maximum(slot - PIECES - 2 * PIECES * both, 0)
        near_d = u // (2 * PIECES) + 1
        near_v = lax.rem(u, 2 * PIECES)
        near_seq = jnp.where(lax.rem(near_v, 2) == 0, b - near_d, b + near_d)
        far_d = both + 1 + v // PIECES
        far_seq = jnp.where(b > n - 1 - b, b - far_d, b + far_d)
        is_own = slot < PIECES
        is_near = slot < PIECES + 2 * PIECES * both
        seq = jnp.where(is_own, b, jnp.where(is_near, near_seq, far_seq))
        piece = jnp.where(is_own, slot, jnp.where(is_near, near_v // 2, lax.rem(v, PIECES)))
        return seq, piece

    def steps_from_root(way, source):
        gap = place - ring(source) if way == 0 else ring(source) - place
        return lax.rem(gap + groups, groups)

    def chain_copy(way, source, piece):
        return pltpu.make_async_remote_copy(
            src_ref=stage.at[way, source, piece], dst_ref=incoming.at[way, source, piece],
            send_sem=c_send.at[way, source, piece], recv_sem=c_recv.at[way, source, piece],
            device_id={"heads": ahead if way == 0 else behind}, device_id_type=MESH,
        )

    def hop(h, slot):
        source, piece = slot_of(slot)
        for way in range(2):
            @pl.when(steps_from_root(way, source) == (h + 1) % groups)
            def _():
                chain_copy(way, source, piece).wait_recv()
                merged = (
                    incoming[way, source, piece].astype(jnp.float32)
                    + stage[way, source, piece].astype(jnp.float32)
                ).astype(jnp.bfloat16)
                if h < groups - 1:
                    stage[way, source, piece] = merged
                    chain_copy(way, source, piece).start()
                else:
                    spot = pl.ds(pl.multiple_of(piece * rows, rows), rows)
                    out_ref[0, spot, way * half:(way + 1) * half] = merged

    def step(i, _):
        @pl.when(i < slots)
        def _():
            source, piece = slot_of(i)

            @pl.when(source != b)
            def _():
                z_copy(0, source, piece).wait_recv()
                pass_on(source, piece)

            spot = pl.ds(pl.multiple_of(piece * rows, rows), rows)
            for way in range(2):
                def tile(t, _):
                    cols = pl.multiple_of(t * COLS, COLS)
                    stage[way, source, piece, :, pl.ds(cols, COLS)] = jnp.dot(
                        gath[source, spot, :],
                        w_ref[:, pl.ds(pl.multiple_of(way * half + cols, COLS), COLS)],
                        preferred_element_type=jnp.float32,
                    ).astype(jnp.bfloat16)
                    return 0

                lax.fori_loop(0, half // COLS, tile, 0)

                @pl.when(steps_from_root(way, source) == 1)
                def _():
                    chain_copy(way, source, piece).start()

        for h in range(1, groups):
            slot = i - h * LAG

            @pl.when((slot >= 0) & (slot < slots))
            def _():
                hop(h, slot)

        return 0

    lax.fori_loop(0, slots + (groups - 1) * LAG, step, 0)

    for d in range(1, reach + 1):
        @pl.when(me + d < seqs)
        def _():
            for copy in kv_copies(d, me + d):
                copy.wait_send()

    def finish(slot, _):
        source, piece = slot // PIECES, lax.rem(slot, PIECES)
        for way in range(2):
            @pl.when(goes(way, source))
            def _():
                z_copy(way, source, piece).wait_send()

            @pl.when(steps_from_root(way, source) != 0)
            def _():
                chain_copy(way, source, piece).wait_send()

        return 0

    lax.fori_loop(0, slots, finish, 0)


def solution(mesh):
    seqs, groups, n = mesh.shape["seq"], mesh.shape["heads"], mesh.shape["batch"]

    def per_device(queries, keys, values, doc_lengths, out_weight):
        shard_len, q_width = queries.shape[1:]
        kv_width = keys.shape[2]
        columns = out_weight.shape[1]
        seq_total = seqs * shard_len
        longest = seq_total // 2 + shard_len // 2
        reach = min((longest + shard_len - 2) // shard_len, seqs - 1)
        rows = shard_len // PIECES
        key_count = (reach + 1) * shard_len
        vmem = pl.BlockSpec(memory_space=pltpu.VMEM)
        dma = pltpu.SemaphoreType.DMA
        return pl.pallas_call(
            functools.partial(kernel, (seqs, groups, n, reach)),
            out_shape=jax.ShapeDtypeStruct((1, shard_len, columns), jnp.bfloat16),
            in_specs=[
                vmem, vmem, vmem,
                pl.BlockSpec(memory_space=pltpu.SMEM),
                pl.BlockSpec(memory_space=pl.ANY),
            ],
            out_specs=vmem,
            scratch_shapes=[
                pltpu.VMEM(out_weight.shape, jnp.bfloat16),
                pltpu.VMEM((key_count, kv_width), jnp.bfloat16),
                pltpu.VMEM((key_count, kv_width), jnp.bfloat16),
                pltpu.VMEM((n, shard_len, q_width), jnp.bfloat16),
                pltpu.VMEM((2, n, PIECES, rows, columns // 2), jnp.bfloat16),
                pltpu.VMEM((2, n, PIECES, rows, columns // 2), jnp.bfloat16),
                dma,
                dma((2, max(reach, 1))),
                dma((2, max(reach, 1))),
                dma((2, n, PIECES)),
                dma((n, PIECES)),
                dma((2, n, PIECES)),
                dma((2, n, PIECES)),
            ],
            compiler_params=pltpu.CompilerParams(
                collective_id=0, has_side_effects=True, vmem_limit_bytes=60 * 2**20
            ),
        )(queries, keys, values, doc_lengths, out_weight)

    return jax.shard_map(
        per_device,
        mesh=mesh,
        in_specs=(
            P("batch", "seq", "heads"),
            P("batch", "seq", "heads"),
            P("batch", "seq", "heads"),
            P("batch", None),
            P("heads", "batch"),
        ),
        out_specs=P("heads", "seq", "batch"),
        check_vma=False,
    )
```

profile of v0, /device:TPU:24, one launch (start us, length us, event | category | flops | bytes accessed | tf_op | source)
XLA Modules:
  0.0 99.6 jit_solution(1584767529388138255)
XLA Ops:
  0.0 97.2 %shard_map.55 = bf16[1,256,2048]{2,1,0:T(8,128)(2,1)} custom-call(bf16[1,256,2048]{2,1,0:T(8,128)(2,1)} %q_ref.1, bf16[1,256,256]{2,1,0:T(8,128)(2,1)} %k_ref.1, bf16[1,256,256]{2,1,0:T(8,128)(2,1)} %v_ref.1, s32[1,16]{1,0:T(1,128)} %len_ref.1, bf16[2048,2048]{1,0:T(8,128)(2,1)} %w_hbm.1), custom_call_target="tpu_custom_call" | custom-call | tf_op jit(solution)/shard_map/pallas_call | solution.py:281
  97.3 2.3 %copy.7 = bf16[1,256,2048]{2,1,0:T(8,128)(2,1)} copy(bf16[1,256,2048]{2,1,0:T(8,128)(2,1)} %shard_map.55) | data formatting | bytes 2097152
where the time goes:
time: 99.7 us; the launch traced here: 99.6 us
  Pallas kernels  97.2 us (97%)
  local copies, waits for them, and re-layouts  2.3 us (2%)
    pallas_call x1, Pallas kernels, per_device(): pl.pallas_call(functools.partial(kernel, (seqs, groups, n, reach)), out_s...  97.2 us
    unnamed x1, local copies, waits for them, and re-layouts  2.3 us

commit v1 on v0

v1 whole, which is shorter than its diff:
```python
import functools
import math

import jax
import jax.numpy as jnp
from jax import lax
from jax.experimental import pallas as pl
from jax.experimental.pallas import tpu as pltpu
from jax.sharding import PartitionSpec as P

HEAD_WIDTH = 128
DOCS = 16
PIECES = 16
AHEAD = 4
LAG = 1
COLS = 512
MESH = pl.DeviceIdType.MESH


def delay(d):
    return jnp.maximum(d - 1, 0)


def kernel(
    sizes, q_hbm, k_hbm, v_hbm, len_hbm, w_hbm, out_ref,
    w_ref, queries, keys, vals, lens, gath, stage, incoming,
    w_sem, load_sem, kv_send, kv_recv, z_send, z_recv, c_send, c_recv,
):
    seqs, groups, n, reach = sizes
    shard_len, q_width = queries.shape
    kv_width = keys.shape[1]
    columns = w_ref.shape[1]
    kv_heads = kv_width // HEAD_WIDTH
    per_kv = q_width // kv_width
    rows = shard_len // PIECES
    blocks = columns // COLS
    own_keys = reach * shard_len

    me = lax.axis_index("seq")
    head = lax.axis_index("heads")
    b = lax.axis_index("batch")

    barrier = pltpu.get_barrier_semaphore()

    def greet(axis, index):
        pl.semaphore_signal(barrier, inc=1, device_id={axis: index}, device_id_type=MESH)

    expected = 0
    for d in range(1, reach + 1):
        for cond, index in ((me >= d, me - d), (me + d < seqs, me + d)):
            expected = expected + cond.astype(jnp.int32)
            pl.when(cond)(functools.partial(greet, "seq", index))
    for cond, index in ((b > 0, b - 1), (b < n - 1, b + 1)):
        expected = expected + cond.astype(jnp.int32)
        pl.when(cond)(functools.partial(greet, "batch", index))
    for d in range(1, groups):
        greet("heads", lax.rem(head + d, groups))
    expected = expected + groups - 1

    first_rows = pl.ds(0, rows)
    other_rows = pl.ds(rows, shard_len - rows)
    own_spot = pl.ds(own_keys, shard_len)
    loads = [
        pltpu.make_async_copy(k_hbm.at[0], keys.at[own_spot], load_sem.at[0]),
        pltpu.make_async_copy(q_hbm.at[0, first_rows], queries.at[first_rows], load_sem.at[1]),
        pltpu.make_async_copy(v_hbm.at[0], vals.at[own_spot], load_sem.at[2]),
        pltpu.make_async_copy(len_hbm, lens, load_sem.at[3]),
        pltpu.make_async_copy(q_hbm.at[0, other_rows], queries.at[other_rows], load_sem.at[4]),
    ]
    for load in loads:
        load.start()
    w_copy = pltpu.make_async_copy(w_hbm, w_ref, w_sem)
    w_copy.start()

    for d in range(1, reach + 1):
        @pl.when((me < d) & (me > 0))
        def _():
            spot = pl.ds((reach - d) * shard_len, shard_len)
            keys[spot, :] = jnp.zeros((shard_len, kv_width), keys.dtype)
            vals[spot, :] = jnp.zeros((shard_len, kv_width), vals.dtype)

    pl.semaphore_wait(barrier, expected)

    def kv_copies(d, target):
        spot = pl.ds((reach - d) * shard_len, shard_len)
        return [
            pltpu.make_async_remote_copy(
                src_ref=src.at[0], dst_ref=dst.at[spot],
                send_sem=kv_send.at[i, d - 1], recv_sem=kv_recv.at[i, d - 1],
                device_id={"seq": target}, device_id_type=MESH,
            )
            for i, (src, dst) in enumerate(((k_hbm, keys), (v_hbm, vals)))
        ]

    for d in range(1, reach + 1):
        @pl.when(me + d < seqs)
        def _():
            for copy in kv_copies(d, me + d):
                copy.start()

    for load in loads[:4]:
        load.wait()
    for d in range(1, reach + 1):
        @pl.when(me >= d)
        def _():
            for copy in kv_copies(d, me - d):
                copy.wait_recv()

    def slot_rows(source):
        return pl.ds(pl.multiple_of(source * rows, rows), rows)

    def z_copy(way, source, piece):
        target = b + 1 if way == 0 else b - 1
        here = piece + delay(jnp.abs(b - source))
        there = piece + delay(jnp.abs(target - source))
        return pltpu.make_async_remote_copy(
            src_ref=gath.at[here, slot_rows(source)],
            dst_ref=gath.at[there, slot_rows(source)],
            send_sem=z_send.at[way, source, piece], recv_sem=z_recv.at[source, piece],
            device_id={"batch": target}, device_id_type=MESH,
        )

    def z_arrival(source, piece):
        spot = gath.at[piece + delay(jnp.abs(b - source)), slot_rows(source)]
        return pltpu.make_async_copy(spot, spot, z_recv.at[source, piece])

    def goes(way, source):
        if way == 0:
            return (source <= b) & (b < n - 1)
        return (source >= b) & (b > 0)

    def pass_on(source, piece):
        for way in range(2):
            @pl.when(goes(way, source))
            def _():
                z_copy(way, source, piece).start()

    rate = HEAD_WIDTH ** (-0.5) * math.log2(math.e)
    shard_start = me * shard_len

    def attend(piece):
        base = pl.multiple_of(piece * rows, rows)
        row_pos = shard_start + base + lax.broadcasted_iota(jnp.int32, (rows, HEAD_WIDTH), 0)
        start = jnp.zeros((rows, HEAD_WIDTH), jnp.int32)
        end = jnp.int32(0)
        for d in range(DOCS):
            end = end + lens[0, d]
            start = jnp.where(row_pos >= end, end, start)

        def over(low):
            count = own_keys + shard_len - low
            key_pos = (
                shard_start - own_keys + low
                + lax.broadcasted_iota(jnp.int32, (rows, count), 1)
            )
            allowed = (key_pos >= start[:, :1]) & (key_pos <= row_pos[:, :1])
            bias = jnp.where(allowed, 0.0, -jnp.inf).astype(jnp.float32)
            bias = jnp.concatenate([bias] * per_kv, axis=0)
            for g in range(kv_heads):
                gcols = slice(g * HEAD_WIDTH, (g + 1) * HEAD_WIDTH)
                q = jnp.concatenate(
                    [
                        queries[pl.ds(base, rows), j * HEAD_WIDTH:(j + 1) * HEAD_WIDTH]
                        for j in range(g * per_kv, (g + 1) * per_kv)
                    ],
                    axis=0,
                )
                scores = lax.dot_general(
                    q, keys[low:, gcols], (((1,), (1,)), ((), ())),
                    preferred_element_type=jnp.float32,
                ) + bias
                weights = jnp.exp2((scores - jnp.max(scores, axis=1, keepdims=True)) * rate)
                total = jnp.sum(weights, axis=1, keepdims=True)
                summed = jnp.dot(
                    weights.astype(jnp.bfloat16), vals[low:, gcols],
                    preferred_element_type=jnp.float32,
                )
                result = (summed / total).astype(jnp.bfloat16)
                for i in range(per_kv):
                    j = g * per_kv + i
                    gath[piece, slot_rows(b), j * HEAD_WIDTH:(j + 1) * HEAD_WIDTH] = (
                        result[i * rows:(i + 1) * rows]
                    )

        if reach > 0:
            pl.when(me == 0)(functools.partial(over, own_keys))
            pl.when(me > 0)(functools.partial(over, 0))
        else:
            over(0)

    def part_copy(source, piece, slot, spot, cols):
        return pltpu.make_async_remote_copy(
            src_ref=stage.at[piece + delay(jnp.abs(b - source)), spot, cols],
            dst_ref=incoming.at[slot, piece, :, cols],
            send_sem=c_send.at[source, piece], recv_sem=c_recv.at[slot, piece],
            device_id={"heads": source}, device_id_type=MESH,
        )

    def part_to(source, piece, cols):
        slot = lax.rem(head - source - 1 + 2 * groups, groups)
        return part_copy(source, piece, slot, slot_rows(source), cols)

    all_cols = pl.ds(0, columns)
    last_delay = delay(jnp.maximum(b, n - 1 - b))

    def arrive(source, valid, piece):
        @pl.when(valid & (piece >= 0) & (piece < PIECES))
        def _():
            z_arrival(source, piece).wait()
            pass_on(source, piece)

    def project(r):
        for d in range(1, n):
            piece = r - max(d - 1, 0)
            arrive(b - d, b >= d, piece)
            arrive(b + d, b + d < n, piece)

        def tile(t, _):
            cols = pl.ds(pl.multiple_of(t * COLS, COLS), COLS)
            stage[r, :, cols] = jnp.dot(
                gath[r], w_ref[:, cols], preferred_element_type=jnp.float32
            ).astype(jnp.bfloat16)
            for source in range(n):
                piece = r - delay(jnp.abs(b - source))

                @pl.when((piece >= 0) & (piece < PIECES) & (head != source))
                def _():
                    part_to(source, piece, cols).start()

            return 0

        lax.fori_loop(0, blocks, tile, 0)

    def collect(piece, r):
        for slot in range(groups - 1):
            spot = incoming.at[slot, piece]
            pltpu.make_async_copy(spot, spot, c_recv.at[slot, piece]).wait()

        def tile(t, _):
            cols = pl.ds(pl.multiple_of(t * COLS, COLS), COLS)
            total = stage[r, slot_rows(head), cols].astype(jnp.float32)
            for slot in range(groups - 1):
                total = total + incoming[slot, piece, :, cols].astype(jnp.float32)
            out_ref[0, slot_rows(piece), cols] = total.astype(jnp.bfloat16)
            return 0

        lax.fori_loop(0, blocks, tile, 0)

    def step(i, _):
        @pl.when(i < PIECES)
        def _():
            @pl.when(i == 1)
            def _():
                loads[4].wait()

            attend(i)
            pass_on(b, i)

        @pl.when(i == AHEAD)
        def _():
            w_copy.wait()

        r = i - AHEAD

        @pl.when((r >= 0) & (r < PIECES + last_delay))
        def _():
            project(r)

        done = r - LAG
        piece = done - delay(jnp.abs(b - head))

        @pl.when((piece >= 0) & (piece < PIECES))
        def _():
            collect(piece, done)

        return 0

    lax.fori_loop(0, AHEAD + PIECES + max(n - 2, 0) + LAG, step, 0)

    for d in range(1, reach + 1):
        @pl.when(me + d < seqs)
        def _():
            for copy in kv_copies(d, me + d):
                copy.wait_send()

    def finish(piece, _):
        for source in range(n):
            for way in range(2):
                @pl.when(goes(way, source))
                def _():
                    z_copy(way, source, piece).wait_send()

            @pl.when(head != source)
            def _():
                part_to(source, piece, all_cols).wait_send()

        return 0

    lax.fori_loop(0, PIECES, finish, 0)


def solution(mesh):
    seqs, groups, n = mesh.shape["seq"], mesh.shape["heads"], mesh.shape["batch"]

    def per_device(queries, keys, values, doc_lengths, out_weight):
        shard_len, q_width = queries.shape[1:]
        kv_width = keys.shape[2]
        columns = out_weight.shape[1]
        seq_total = seqs * shard_len
        longest = seq_total // 2 + shard_len // 2
        reach = min((longest + shard_len - 2) // shard_len, seqs - 1)
        rows = shard_len // PIECES
        rounds = PIECES + max(n - 2, 0)
        key_count = (reach + 1) * shard_len
        hbm = pl.BlockSpec(memory_space=pltpu.HBM)
        dma = pltpu.SemaphoreType.DMA
        return pl.pallas_call(
            functools.partial(kernel, (seqs, groups, n, reach)),
            out_shape=jax.ShapeDtypeStruct((1, shard_len, columns), jnp.bfloat16),
            in_specs=[hbm] * 5,
            out_specs=pl.BlockSpec(memory_space=pltpu.VMEM),
            scratch_shapes=[
                pltpu.VMEM(out_weight.shape, jnp.bfloat16),
                pltpu.VMEM((shard_len, q_width), jnp.bfloat16),
                pltpu.VMEM((key_count, kv_width), jnp.bfloat16),
                pltpu.VMEM((key_count, kv_width), jnp.bfloat16),
                pltpu.SMEM(doc_lengths.shape, jnp.int32),
                pltpu.VMEM((rounds, n * rows, q_width), jnp.bfloat16),
                pltpu.VMEM((rounds, n * rows, columns), jnp.bfloat16),
                pltpu.VMEM((groups - 1, PIECES, rows, columns), jnp.bfloat16),
                dma,
                dma((5,)),
                dma((2, max(reach, 1))),
                dma((2, max(reach, 1))),
                dma((2, n, PIECES)),
                dma((n, PIECES)),
                dma((n, PIECES)),
                dma((groups - 1, PIECES)),
            ],
            compiler_params=pltpu.CompilerParams(
                collective_id=0, has_side_effects=True, vmem_limit_bytes=int(60 * 2**20)
            ),
        )(queries, keys, values, doc_lengths, out_weight)

    return jax.shard_map(
        per_device,
        mesh=mesh,
        in_specs=(
            P("batch", "seq", "heads"),
            P("batch", "seq", "heads"),
            P("batch", "seq", "heads"),
            P("batch", None),
            P("heads", "batch"),
        ),
        out_specs=P("heads", "seq", "batch"),
        check_vma=False,
    )
```

time: 99.7 us -> 87.8 us (0.88)
  the two profiles are of different devices: /device:TPU:24 before, /device:TPU:1 now
where the time goes in v1:
time: 87.8 us; the launch traced here: 86.5 us
  Pallas kernels  84.2 us (96%)
  local copies, waits for them, and re-layouts  2.3 us (3%)
    pallas_call x1, Pallas kernels, per_device(): pl.pallas_call(functools.partial(kernel, (seqs, groups, n, reach)), out_s...  84.2 us
    unnamed x1, local copies, waits for them, and re-layouts  2.3 us

profile of v1, /device:TPU:1, one launch (start us, length us, event | category | flops | bytes accessed | tf_op | source)
XLA Modules:
  0.0 86.5 jit_solution(13120600767877929438)
XLA Ops:
  0.0 84.2 %shard_map.55 = bf16[1,256,2048]{2,1,0:T(8,128)(2,1)} custom-call(bf16[1,256,2048]{2,1,0:T(8,128)(2,1)} %q_hbm.1, bf16[1,256,256]{2,1,0:T(8,128)(2,1)} %k_hbm.1, bf16[1,256,256]{2,1,0:T(8,128)(2,1)} %v_hbm.1, s32[1,16]{1,0:T(1,128)} %len_hbm.1, bf16[2048,2048]{1,0:T(8,128)(2,1)} %w_hbm.1), custom_call_target="tpu_custom_call" | custom-call | tf_op jit(solution)/shard_map/pallas_call | solution.py:317
  84.2 2.3 %copy.7 = bf16[1,256,2048]{2,1,0:T(8,128)(2,1)} copy(bf16[1,256,2048]{2,1,0:T(8,128)(2,1)} %shard_map.55) | data formatting | bytes 2097152

commit v2 on v1

--- a/solution.py
+++ b/solution.py
@@ -11,19 +11,15 @@
 HEAD_WIDTH = 128
 DOCS = 16
 PIECES = 16
-AHEAD = 4
-LAG = 1
-COLS = 512
+HOP = 2
+COLS = 1024
+PARTS = 4
 MESH = pl.DeviceIdType.MESH
-
-
-def delay(d):
-    return jnp.maximum(d - 1, 0)
 
 
 def kernel(
     sizes, q_hbm, k_hbm, v_hbm, len_hbm, w_hbm, out_ref,
-    w_ref, queries, keys, vals, lens, gath, stage, incoming,
+    w_ref, queries, keys, vals, lens, gath, stage, incoming, acc,
     w_sem, load_sem, kv_send, kv_recv, z_send, z_recv, c_send, c_recv,
 ):
     seqs, groups, n, reach = sizes
@@ -33,7 +29,7 @@
     kv_heads = kv_width // HEAD_WIDTH
     per_kv = q_width // kv_width
     rows = shard_len // PIECES
-    blocks = columns // COLS
+    pair = 2 * rows
     own_keys = reach * shard_len
 
     me = lax.axis_index("seq")
@@ -106,34 +102,58 @@
             for copy in kv_copies(d, me - d):
                 copy.wait_recv()
 
-    def slot_rows(source):
-        return pl.ds(pl.multiple_of(source * rows, rows), rows)
-
-    def z_copy(way, source, piece):
-        target = b + 1 if way == 0 else b - 1
-        here = piece + delay(jnp.abs(b - source))
-        there = piece + delay(jnp.abs(target - source))
+    deep = q_width // PARTS
+    every = pl.ds(0, q_width)
+    last = PIECES - 1
+
+    def part_cols(part):
+        return pl.ds(part * deep, deep)
+
+    def pair_rows(index):
+        return pl.ds(pl.multiple_of(index * pair, pair), pair)
+
+    def piece_rows(piece):
+        return pl.ds(pl.multiple_of(piece * rows, rows), rows)
+
+    def place(source, piece):
+        row = source * pair + lax.rem(piece, 2) * rows
+        return lax.div(piece, 2), pl.ds(pl.multiple_of(row, rows), rows)
+
+    def z_copy(way, source, piece, index, cols):
+        spot = gath.at[*place(source, piece), cols]
         return pltpu.make_async_remote_copy(
-            src_ref=gath.at[here, slot_rows(source)],
-            dst_ref=gath.at[there, slot_rows(source)],
-            send_sem=z_send.at[way, source, piece], recv_sem=z_recv.at[source, piece],
-            device_id={"batch": target}, device_id_type=MESH,
+            src_ref=spot, dst_ref=spot,
+            send_sem=z_send.at[way, source], recv_sem=z_recv.at[source, index],
+            device_id={"batch": b + 1 if way == 0 else b - 1}, device_id_type=MESH,
         )
 
-    def z_arrival(source, piece):
-        spot = gath.at[piece + delay(jnp.abs(b - source)), slot_rows(source)]
-        return pltpu.make_async_copy(spot, spot, z_recv.at[source, piece])
+    def z_wait(source, piece, index, cols):
+        spot = gath.at[*place(source, piece), cols]
+        pltpu.make_async_copy(spot, spot, z_recv.at[source, index]).wait()
 
     def goes(way, source):
         if way == 0:
             return (source <= b) & (b < n - 1)
         return (source >= b) & (b > 0)
 
-    def pass_on(source, piece):
-        for way in range(2):
-            @pl.when(goes(way, source))
-            def _():
-                z_copy(way, source, piece).start()
+    def move(way, source, piece, cond, own):
+        cond = cond & goes(way, source) & (source >= 0) & (source < n)
+
+        def go(index, cols):
+            if not own:
+                z_wait(source, piece, index, cols)
+            z_copy(way, source, piece, index, cols).start()
+
+        @pl.when(cond & (piece >= 0) & (piece < last))
+        def _():
+            go(piece, every)
+
+        late = b == (n - 2 if way == 0 else 1)
+
+        @pl.when(cond & (piece == last) & jnp.logical_not(late))
+        def _():
+            for part in range(PARTS):
+                go(last + part, part_cols(part))
 
     rate = HEAD_WIDTH ** (-0.5) * math.log2(math.e)
     shard_start = me * shard_len
@@ -178,7 +198,7 @@
                 result = (summed / total).astype(jnp.bfloat16)
                 for i in range(per_kv):
                     j = g * per_kv + i
-                    gath[piece, slot_rows(b), j * HEAD_WIDTH:(j + 1) * HEAD_WIDTH] = (
+                    gath[*place(b, piece), j * HEAD_WIDTH:(j + 1) * HEAD_WIDTH] = (
                         result[i * rows:(i + 1) * rows]
                     )
 
@@ -188,63 +208,108 @@
         else:
             over(0)
 
-    def part_copy(source, piece, slot, spot, cols):
-        return pltpu.make_async_remote_copy(
-            src_ref=stage.at[piece + delay(jnp.abs(b - source)), spot, cols],
-            dst_ref=incoming.at[slot, piece, :, cols],
-            send_sem=c_send.at[source, piece], recv_sem=c_recv.at[slot, piece],
-            device_id={"heads": source}, device_id_type=MESH,
-        )
-
-    def part_to(source, piece, cols):
+    at_end = (b == 0) | (b == n - 1)
+
+    def part_send(source, index, here, there, sem, cols):
         slot = lax.rem(head - source - 1 + 2 * groups, groups)
-        return part_copy(source, piece, slot, slot_rows(source), cols)
-
-    all_cols = pl.ds(0, columns)
-    last_delay = delay(jnp.maximum(b, n - 1 - b))
-
-    def arrive(source, valid, piece):
-        @pl.when(valid & (piece >= 0) & (piece < PIECES))
-        def _():
-            z_arrival(source, piece).wait()
-            pass_on(source, piece)
-
-    def project(r):
-        for d in range(1, n):
-            piece = r - max(d - 1, 0)
-            arrive(b - d, b >= d, piece)
-            arrive(b + d, b + d < n, piece)
-
+
+        @pl.when(head != source)
+        def _():
+            pltpu.make_async_remote_copy(
+                src_ref=stage.at[index, here, cols],
+                dst_ref=incoming.at[slot, there, cols],
+                send_sem=c_send.at[source], recv_sem=c_recv.at[slot, sem],
+                device_id={"heads": source}, device_id_type=MESH,
+            ).start()
+
+    def over_tiles(body, width=COLS):
         def tile(t, _):
-            cols = pl.ds(pl.multiple_of(t * COLS, COLS), COLS)
-            stage[r, :, cols] = jnp.dot(
-                gath[r], w_ref[:, cols], preferred_element_type=jnp.float32
-            ).astype(jnp.bfloat16)
+            body(pl.ds(pl.multiple_of(t * width, width), width))
+            return 0
+
+        lax.fori_loop(0, columns // width, tile, 0)
+
+    def product(lhs, depth, cols):
+        return jnp.dot(lhs, w_ref[depth, cols], preferred_element_type=jnp.float32)
+
+    def project_pair(index):
+        for source in range(n):
+            @pl.when(at_end & (source != b))
+            def _():
+                z_wait(source, 2 * index, 2 * index, every)
+                z_wait(source, 2 * index + 1, 2 * index + 1, every)
+
+        def body(cols):
+            stage[index, :, cols] = product(gath[index], every, cols).astype(jnp.bfloat16)
             for source in range(n):
-                piece = r - delay(jnp.abs(b - source))
-
-                @pl.when((piece >= 0) & (piece < PIECES) & (head != source))
+                spot = pl.ds(source * pair, pair)
+                part_send(source, index, spot, pair_rows(index), index, cols)
+
+        over_tiles(body)
+
+    half = PIECES // 2 - 1
+
+    def spots(piece):
+        return [pl.ds(s * pair + (piece % 2) * rows, rows) for s in range(n)]
+
+    def project_one():
+        piece = last - 1
+        for source in range(n):
+            @pl.when(at_end & (source != b))
+            def _():
+                z_wait(source, piece, piece, every)
+
+        def body(cols):
+            lhs = jnp.concatenate([gath[half, spot, :] for spot in spots(piece)], axis=0)
+            part = product(lhs, every, cols).astype(jnp.bfloat16)
+            for source, spot in enumerate(spots(piece)):
+                stage[half, spot, cols] = part[source * rows:(source + 1) * rows]
+                part_send(source, half, spot, pl.ds(piece * rows, rows), half, cols)
+
+        over_tiles(body)
+
+    def project_last():
+        for part in range(PARTS):
+            for source in range(n):
+                @pl.when(at_end & (source != b))
                 def _():
-                    part_to(source, piece, cols).start()
-
-            return 0
-
-        lax.fori_loop(0, blocks, tile, 0)
-
-    def collect(piece, r):
+                    z_wait(source, last, last + part, part_cols(part))
+
+            def body(cols):
+                lhs = jnp.concatenate(
+                    [gath[half, spot, part_cols(part)] for spot in spots(last)], axis=0
+                )
+                total = product(lhs, part_cols(part), cols)
+                if part > 0:
+                    total = total + acc[:, cols]
+                if part < PARTS - 1:
+                    acc[:, cols] = total
+                    return
+                total = total.astype(jnp.bfloat16)
+                for source, spot in enumerate(spots(last)):
+                    stage[half, spot, cols] = total[source * rows:(source + 1) * rows]
+                    part_send(source, half, spot, pl.ds(last * rows, rows), half + 1, cols)
+
+            over_tiles(body, COLS if part == PARTS - 1 else 2 * COLS)
+
+    def collect(index, here, there, sem):
         for slot in range(groups - 1):
-            spot = incoming.at[slot, piece]
-            pltpu.make_async_copy(spot, spot, c_recv.at[slot, piece]).wait()
-
-        def tile(t, _):
-            cols = pl.ds(pl.multiple_of(t * COLS, COLS), COLS)
-            total = stage[r, slot_rows(head), cols].astype(jnp.float32)
+            spot = incoming.at[slot, there]
+            pltpu.make_async_copy(spot, spot, c_recv.at[slot, sem]).wait()
+
+        def body(cols):
+            total = stage[index, here, cols].astype(jnp.float32)
             for slot in range(groups - 1):
-                total = total + incoming[slot, piece, :, cols].astype(jnp.float32)
-            out_ref[0, slot_rows(piece), cols] = total.astype(jnp.bfloat16)
-            return 0
-
-        lax.fori_loop(0, blocks, tile, 0)
+                total = total + incoming[slot, there, cols].astype(jnp.float32)
+            out_ref[0, there, cols] = total.astype(jnp.bfloat16)
+
+        over_tiles(body)
+
+    def collect_one(piece, sem):
+        collect(*place(head, piece), piece_rows(piece), sem)
+
+    behind = (n - 1) * HOP
+    hold = (n - 2) * HOP
 
     def step(i, _):
         @pl.when(i < PIECES)
@@ -254,28 +319,62 @@
                 loads[4].wait()
 
             attend(i)
-            pass_on(b, i)
-
-        @pl.when(i == AHEAD)
+
+        for way in range(2):
+            late = b == (n - 2 if way == 0 else 1)
+            for d in range(n - 1):
+                source = b - d if way == 0 else b + d
+                begin = hold + sum(hold - e * HOP for e in range(d))
+                early = i - d * HOP
+                kept = i - hold
+                move(
+                    way, source, early,
+                    jnp.logical_not(late) | (i < begin) | (d == n - 2), d == 0,
+                )
+                if d < n - 2:
+                    move(
+                        way, source, kept,
+                        late & (kept >= begin - d * HOP) & (kept < last), d == 0,
+                    )
+
+            @pl.when(late & (i == last + hold))
+            def _():
+                for part in range(PARTS):
+                    for d in range(n - 1):
+                        source = b - d if way == 0 else b + d
+                        if d > 0:
+                            z_wait(source, last, last + part, part_cols(part))
+                        z_copy(way, source, last, last + part, part_cols(part)).start()
+
+        @pl.when(i == behind)
         def _():
             w_copy.wait()
 
-        r = i - AHEAD
-
-        @pl.when((r >= 0) & (r < PIECES + last_delay))
-        def _():
-            project(r)
-
-        done = r - LAG
-        piece = done - delay(jnp.abs(b - head))
-
-        @pl.when((piece >= 0) & (piece < PIECES))
-        def _():
-            collect(piece, done)
+        r = i - behind
+        odd = lax.rem(jnp.maximum(r, 0), 2) == 1
+        index = lax.div(jnp.maximum(r, 0), 2)
+
+        @pl.when(odd & (r < last))
+        def _():
+            project_pair(index)
+
+        @pl.when(r == last - 1)
+        def _():
+            project_one()
+
+        @pl.when(r == last)
+        def _():
+            project_last()
+
+        @pl.when(odd & (r >= 3) & (r <= last))
+        def _():
+            collect(index - 1, pair_rows(head), pair_rows(index - 1), index - 1)
 
         return 0
 
-    lax.fori_loop(0, AHEAD + PIECES + max(n - 2, 0) + LAG, step, 0)
+    lax.fori_loop(0, behind + PIECES, step, 0)
+    collect_one(last - 1, half)
+    collect_one(last, half + 1)
 
     for d in range(1, reach + 1):
         @pl.when(me + d < seqs)
@@ -283,20 +382,18 @@
             for copy in kv_copies(d, me + d):
                 copy.wait_send()
 
-    def finish(piece, _):
-        for source in range(n):
-            for way in range(2):
-                @pl.when(goes(way, source))
-                def _():
-                    z_copy(way, source, piece).wait_send()
-
-            @pl.when(head != source)
+    def drain(like, sem):
+        pltpu.make_async_copy(like, like, sem).wait()
+
+    for source in range(n):
+        for way in range(2):
+            @pl.when(goes(way, source))
             def _():
-                part_to(source, piece, all_cols).wait_send()
-
-        return 0
-
-    lax.fori_loop(0, PIECES, finish, 0)
+                drain(queries, z_send.at[way, source])
+
+        @pl.when(head != source)
+        def _():
+            drain(out_ref.at[0], c_send.at[source])
 
 
 def solution(mesh):
@@ -310,13 +407,13 @@
         longest = seq_total // 2 + shard_len // 2
         reach = min((longest + shard_len - 2) // shard_len, seqs - 1)
         rows = shard_len // PIECES
-        rounds = PIECES + max(n - 2, 0)
+        pairs = PIECES // 2
         key_count = (reach + 1) * shard_len
         hbm = pl.BlockSpec(memory_space=pltpu.HBM)
         dma = pltpu.SemaphoreType.DMA
         return pl.pallas_call(
             functools.partial(kernel, (seqs, groups, n, reach)),
-            out_shape=jax.ShapeDtypeStruct((1, shard_len, columns), jnp.bfloat16),
+            out_shape=pltpu.VMEM((1, shard_len, columns), jnp.bfloat16),
             in_specs=[hbm] * 5,
             out_specs=pl.BlockSpec(memory_space=pltpu.VMEM),
             scratch_shapes=[
@@ -325,22 +422,26 @@
                 pltpu.VMEM((key_count, kv_width), jnp.bfloat16),
                 pltpu.VMEM((key_count, kv_width), jnp.bfloat16),
                 pltpu.SMEM(doc_lengths.shape, jnp.int32),
-                pltpu.VMEM((rounds, n * rows, q_width), jnp.bfloat16),
-                pltpu.VMEM((rounds, n * rows, columns), jnp.bfloat16),
-                pltpu.VMEM((groups - 1, PIECES, rows, columns), jnp.bfloat16),
+                pltpu.VMEM((pairs, 2 * n * rows, q_width), jnp.bfloat16),
+                pltpu.VMEM((pairs, 2 * n * rows, columns), jnp.bfloat16),
+                pltpu.VMEM((groups - 1, shard_len, columns), jnp.bfloat16),
+                pltpu.VMEM((n * rows, columns), jnp.float32),
                 dma,
                 dma((5,)),
                 dma((2, max(reach, 1))),
                 dma((2, max(reach, 1))),
-                dma((2, n, PIECES)),
-                dma((n, PIECES)),
-                dma((n, PIECES)),
-                dma((groups - 1, PIECES)),
+                dma((2, n)),
+                dma((n, PIECES - 1 + PARTS)),
+                dma((n,)),
+                dma((groups - 1, pairs + 1)),
             ],
             compiler_params=pltpu.CompilerParams(
-                collective_id=0, has_side_effects=True, vmem_limit_bytes=int(60 * 2**20)
+                collective_id=0, has_side_effects=True, vmem_limit_bytes=48 * 2**20
             ),
-        )(queries, keys, values, doc_lengths, out_weight)
+        )(*(
+            pltpu.with_memory_space_constraint(x, pltpu.HBM)
+            for x in (queries, keys, values, doc_lengths, out_weight)
+        ))
 
     return jax.shard_map(
         per_device,

time: 87.8 us -> 84.4 us (0.961)
  Pallas kernels: 84.2 us -> 82.7 us
  local copies, waits for them, and re-layouts: 2.3 us -> 0.97 us
    pallas_call x1, Pallas kernels: 84.2 us -> 82.7 us  [per_device(): pl.pallas_call(functools.partial(kernel, (seqs, groups, n, reach)), out_s...]
    unnamed x1, local copies, waits for them, and re-layouts: 2.3 us -> 0.97 us
where the time goes in v2:
time: 84.4 us; the launch traced here: 83.7 us
  Pallas kernels  82.7 us (98%)
  local copies, waits for them, and re-layouts  0.97 us (1%)
    pallas_call x1, Pallas kernels, per_device(): pl.pallas_call(functools.partial(kernel, (seqs, groups, n, reach)), out_s...  82.7 us

profile of v2, /device:TPU:1, one launch (start us, length us, event | category | flops | bytes accessed | tf_op | source)
XLA Modules:
  0.0 83.7 jit_solution(1953683666377563490)
XLA Ops:
  0.0 82.7 %shard_map.55 = bf16[1,256,2048]{2,1,0:T(8,128)(2,1)S(1)} custom-call(bf16[1,256,2048]{2,1,0:T(8,128)(2,1)} %q_hbm.1, bf16[1,256,256]{2,1,0:T(8,128)(2,1)} %k_hbm.1, bf16[1,256,256]{2,1,0:T(8,128)(2,1)} %v_hbm.1, s32[1,16]{1,0:T(1,128)} %len_hbm.1, bf16[2048,2048]{1,0:T(8,128)(2,1)} %w_hbm.1), custom_call_target="tpu_custom_call" | custom-call | tf_op jit(solution)/shard_map/pallas_call | solution.py:414
  82.7 1.0 %copy.7 = bf16[1,256,2048]{2,1,0:T(8,128)(2,1)} copy(bf16[1,256,2048]{2,1,0:T(8,128)(2,1)S(1)} %shard_map.55) | data formatting | bytes 2097152

commit v3 on v2

--- a/solution.py
+++ b/solution.py
@@ -41,17 +41,16 @@
     def greet(axis, index):
         pl.semaphore_signal(barrier, inc=1, device_id={axis: index}, device_id_type=MESH)
 
-    expected = 0
+    for d in range(groups - 1, 0, -1):
+        greet("heads", lax.rem(head + d, groups))
+    expected = groups - 1
+    for cond, index in ((b > 0, b - 1), (b < n - 1, b + 1)):
+        expected = expected + cond.astype(jnp.int32)
+        pl.when(cond)(functools.partial(greet, "batch", index))
     for d in range(1, reach + 1):
         for cond, index in ((me >= d, me - d), (me + d < seqs, me + d)):
             expected = expected + cond.astype(jnp.int32)
             pl.when(cond)(functools.partial(greet, "seq", index))
-    for cond, index in ((b > 0, b - 1), (b < n - 1, b + 1)):
-        expected = expected + cond.astype(jnp.int32)
-        pl.when(cond)(functools.partial(greet, "batch", index))
-    for d in range(1, groups):
-        greet("heads", lax.rem(head + d, groups))
-    expected = expected + groups - 1
 
     first_rows = pl.ds(0, rows)
     other_rows = pl.ds(rows, shard_len - rows)
@@ -75,33 +74,6 @@
             keys[spot, :] = jnp.zeros((shard_len, kv_width), keys.dtype)
             vals[spot, :] = jnp.zeros((shard_len, kv_width), vals.dtype)
 
-    pl.semaphore_wait(barrier, expected)
-
-    def kv_copies(d, target):
-        spot = pl.ds((reach - d) * shard_len, shard_len)
-        return [
-            pltpu.make_async_remote_copy(
-                src_ref=src.at[0], dst_ref=dst.at[spot],
-                send_sem=kv_send.at[i, d - 1], recv_sem=kv_recv.at[i, d - 1],
-                device_id={"seq": target}, device_id_type=MESH,
-            )
-            for i, (src, dst) in enumerate(((k_hbm, keys), (v_hbm, vals)))
-        ]
-
-    for d in range(1, reach + 1):
-        @pl.when(me + d < seqs)
-        def _():
-            for copy in kv_copies(d, me + d):
-                copy.start()
-
-    for load in loads[:4]:
-        load.wait()
-    for d in range(1, reach + 1):
-        @pl.when(me >= d)
-        def _():
-            for copy in kv_copies(d, me - d):
-                copy.wait_recv()
-
     deep = q_width // PARTS
     every = pl.ds(0, q_width)
     last = PIECES - 1
@@ -167,8 +139,8 @@
             end = end + lens[0, d]
             start = jnp.where(row_pos >= end, end, start)
 
-        def over(low):
-            count = own_keys + shard_len - low
+        def over(low, high):
+            count = high - low
             key_pos = (
                 shard_start - own_keys + low
                 + lax.broadcasted_iota(jnp.int32, (rows, count), 1)
@@ -186,13 +158,13 @@
                     axis=0,
                 )
                 scores = lax.dot_general(
-                    q, keys[low:, gcols], (((1,), (1,)), ((), ())),
+                    q, keys[low:high, gcols], (((1,), (1,)), ((), ())),
                     preferred_element_type=jnp.float32,
                 ) + bias
                 weights = jnp.exp2((scores - jnp.max(scores, axis=1, keepdims=True)) * rate)
                 total = jnp.sum(weights, axis=1, keepdims=True)
                 summed = jnp.dot(
-                    weights.astype(jnp.bfloat16), vals[low:, gcols],
+                    weights.astype(jnp.bfloat16), vals[low:high, gcols],
                     preferred_element_type=jnp.float32,
                 )
                 result = (summed / total).astype(jnp.bfloat16)
@@ -202,11 +174,47 @@
                         result[i * rows:(i + 1) * rows]
                     )
 
-        if reach > 0:
-            pl.when(me == 0)(functools.partial(over, own_keys))
-            pl.when(me > 0)(functools.partial(over, 0))
-        else:
-            over(0)
+        middle, top = own_keys + shard_len // 2, own_keys + shard_len
+        if isinstance(piece, int):
+            over(own_keys, middle)
+            return
+        soon = piece < PIECES // 2
+        for cond, high in ((soon, middle), (jnp.logical_not(soon), top)):
+            pl.when(cond & (me == 0))(functools.partial(over, own_keys, high))
+            if reach > 0:
+                pl.when(cond & (me > 0))(functools.partial(over, 0, high))
+
+    for load in loads[:4]:
+        load.wait()
+
+    @pl.when(me == 0)
+    def _():
+        attend(0)
+
+    pl.semaphore_wait(barrier, expected)
+
+    def kv_copies(d, target):
+        spot = pl.ds((reach - d) * shard_len, shard_len)
+        return [
+            pltpu.make_async_remote_copy(
+                src_ref=src.at[0], dst_ref=dst.at[spot],
+                send_sem=kv_send.at[i, d - 1], recv_sem=kv_recv.at[i, d - 1],
+                device_id={"seq": target}, device_id_type=MESH,
+            )
+            for i, (src, dst) in enumerate(((k_hbm, keys), (v_hbm, vals)))
+        ]
+
+    for d in range(1, reach + 1):
+        @pl.when(me + d < seqs)
+        def _():
+            for copy in kv_copies(d, me + d):
+                copy.start()
+
+    for d in range(1, reach + 1):
+        @pl.when(me >= d)
+        def _():
+            for copy in kv_copies(d, me - d):
+                copy.wait_recv()
 
     at_end = (b == 0) | (b == n - 1)
 
@@ -318,7 +326,9 @@
             def _():
                 loads[4].wait()
 
-            attend(i)
+            @pl.when((i > 0) | (me > 0))
+            def _():
+                attend(i)
 
         for way in range(2):
             late = b == (n - 2 if way == 0 else 1)

time: 84.4 us -> 82.5 us (0.977)
  Pallas kernels: 82.7 us -> 81.4 us
    pallas_call x1, Pallas kernels: 82.7 us -> 81.4 us  [per_device(): pl.pallas_call(functools.partial(kernel, (seqs, groups, n, reach)), out_s...]
where the time goes in v3:
time: 82.5 us; the launch traced here: 82.3 us
  Pallas kernels  81.4 us (99%)
  local copies, waits for them, and re-layouts  0.97 us (1%)
    pallas_call x1, Pallas kernels, per_device(): pl.pallas_call(functools.partial(kernel, (seqs, groups, n, reach)), out_s...  81.4 us

profile of v3, /device:TPU:1, one launch (start us, length us, event | category | flops | bytes accessed | tf_op | source)
XLA Modules:
  0.0 82.3 jit_solution(16501402382736564745)
XLA Ops:
  0.0 81.4 %shard_map.55 = bf16[1,256,2048]{2,1,0:T(8,128)(2,1)S(1)} custom-call(bf16[1,256,2048]{2,1,0:T(8,128)(2,1)} %q_hbm.1, bf16[1,256,256]{2,1,0:T(8,128)(2,1)} %k_hbm.1, bf16[1,256,256]{2,1,0:T(8,128)(2,1)} %v_hbm.1, s32[1,16]{1,0:T(1,128)} %len_hbm.1, bf16[2048,2048]{1,0:T(8,128)(2,1)} %w_hbm.1), custom_call_target="tpu_custom_call" | custom-call | tf_op jit(solution)/shard_map/pallas_call | solution.py:424
  81.4 1.0 %copy.7 = bf16[1,256,2048]{2,1,0:T(8,128)(2,1)} copy(bf16[1,256,2048]{2,1,0:T(8,128)(2,1)S(1)} %shard_map.55) | data formatting | bytes 2097152

commit v4 on v3

--- a/solution.py
+++ b/solution.py
@@ -65,7 +65,6 @@
     for load in loads:
         load.start()
     w_copy = pltpu.make_async_copy(w_hbm, w_ref, w_sem)
-    w_copy.start()
 
     for d in range(1, reach + 1):
         @pl.when((me < d) & (me > 0))
@@ -216,6 +215,7 @@
             for copy in kv_copies(d, me - d):
                 copy.wait_recv()
 
+    w_copy.start()
     at_end = (b == 0) | (b == n - 1)
 
     def part_send(source, index, here, there, sem, cols):

time: 82.5 us -> 82.5 us (level)
  no operation moved by 1% of the time
where the time goes in v4:
time: 82.5 us; the launch traced here: 82.3 us
  Pallas kernels  81.3 us (99%)
  local copies, waits for them, and re-layouts  0.97 us (1%)
    pallas_call x1, Pallas kernels, per_device(): pl.pallas_call(functools.partial(kernel, (seqs, groups, n, reach)), out_s...  81.3 us

profile of v4, /device:TPU:1, one launch (start us, length us, event | category | flops | bytes accessed | tf_op | source)
XLA Modules:
  0.0 82.3 jit_solution(18015131799627066422)
XLA Ops:
  0.0 81.3 %shard_map.55 = bf16[1,256,2048]{2,1,0:T(8,128)(2,1)S(1)} custom-call(bf16[1,256,2048]{2,1,0:T(8,128)(2,1)} %q_hbm.1, bf16[1,256,256]{2,1,0:T(8,128)(2,1)} %k_hbm.1, bf16[1,256,256]{2,1,0:T(8,128)(2,1)} %v_hbm.1, s32[1,16]{1,0:T(1,128)} %len_hbm.1, bf16[2048,2048]{1,0:T(8,128)(2,1)} %w_hbm.1), custom_call_target="tpu_custom_call" | custom-call | tf_op jit(solution)/shard_map/pallas_call | solution.py:424
  81.4 1.0 %copy.7 = bf16[1,256,2048]{2,1,0:T(8,128)(2,1)} copy(bf16[1,256,2048]{2,1,0:T(8,128)(2,1)S(1)} %shard_map.55) | data formatting | bytes 2097152
